TPU v7x, 32 devices: a whole 2x2x4 slice. The times are simulated.
32 devices in a mesh: cuts: 8 (over z, x), mode: 4 (over y, core).
Axes of the slice: x: 2, y: 2, z: 4, core: 2. Of those that a mesh axis runs over, the one named last changes fastest.
Arguments:
- sliced_state: bfloat16 [8, 16, 4, 128, 2, 128], P(None, 'cuts', None, 'mode'), may hold values from -0.75 to 0.75
- gate_blocks: bfloat16 [32, 2, 128, 128], P('cuts'), may hold values from -0.375 to 0.375
- gate_slot: int32 [32], replicated, may hold values from 0 to 31, each once
- samples: int32 [8, 4096], replicated, may hold values from 0 to 65535
Outputs:
- amplitudes: float32 [32, 128, 2, 128], P('cuts', 'mode')
- sample_probs: float32 [8, 4096], replicated
- xeb_score: float32 [8], replicated
Inputs may be any that keep to these rules, and one draw needn't show every extreme that they name: `gate_slot`: a permutation: every gate block has its own row of gate_blocks. `samples`: flat index s * 128 * 128 + p * 128 + q.
All inputs are finite; a program needn't handle non-finite values.
Results may differ from a plain program's by a relative error of at most 0.022.
Values may be sent and summed in bfloat16 or wider, within the bound.
A program may use at most 64 MiB of HBM per device.

v0:
```python
import jax
import jax.numpy as jnp
from jax import lax
from jax.sharding import PartitionSpec as P


def from_root(array, axis, root):
    mine = lax.axis_index(axis) == root
    return lax.psum(jnp.where(mine, array, jnp.zeros_like(array)), axis)


def apply_gates(tensor, blocks):
    real_part = blocks[:, 0]
    imag_part = blocks[:, 1]
    stacked = jnp.concatenate(
        [
            jnp.concatenate([real_part, imag_part], axis=2),
            jnp.concatenate([-imag_part, real_part], axis=2),
        ],
        axis=1,
    )
    layout = tensor.shape
    flattened = tensor.reshape(layout[0], -1, 2 * layout[-1])
    product = jnp.einsum("crk,ckn->crn", flattened, stacked, preferred_element_type=jnp.float32)
    return product.astype(jnp.bfloat16).reshape(layout)


def select_rows(table, wanted):
    count = table.shape[0]
    onehot = (wanted[:, None] == jnp.arange(count, dtype=jnp.int32)[None, :]).astype(table.dtype)
    picked = jnp.dot(onehot, table.reshape(count, -1), preferred_element_type=jnp.float32)
    return picked.astype(table.dtype).reshape((wanted.shape[0],) + table.shape[1:])


def on_device(sliced_state, gate_blocks, gate_slot, samples):
    circuits = sliced_state.shape[0]
    spectator = sliced_state.shape[2]
    width = sliced_state.shape[5]
    held_count = gate_blocks.shape[0]
    layer_count = gate_slot.shape[0] // (2 * circuits)
    circuit_ids = jnp.arange(circuits, dtype=jnp.int32)
    tensor = lax.all_to_all(sliced_state, "mode", split_axis=0, concat_axis=3, tiled=True)
    local_count = tensor.shape[0]
    local_ids = lax.axis_index("mode") * local_count + jnp.arange(local_count, dtype=jnp.int32)

    def fetch_one(position):
        held_block = select_rows(gate_blocks, jnp.reshape(position % held_count, (1,)))[0]
        return from_root(held_block, "cuts", position // held_count)

    def fetch_gates(layer_index, gate_kind):
        fetched = []
        for circuit in range(local_count):
            fetched.append(
                fetch_one(
                    gate_slot[(local_ids[circuit] * layer_count + layer_index) * 2 + gate_kind]
                )
            )
        return jnp.stack(fetched, axis=0)

    for layer_index in range(layer_count):
        tensor = apply_gates(tensor, fetch_gates(layer_index, 0))
        tensor = jnp.swapaxes(tensor, 3, 5)
        tensor = apply_gates(tensor, fetch_gates(layer_index, 1))
        tensor = jnp.swapaxes(tensor, 3, 5)
    summed = jnp.sum(tensor.astype(jnp.float32), axis=1)
    summed = lax.all_to_all(
        summed.astype(jnp.bfloat16), "mode", split_axis=2, concat_axis=0, tiled=True
    ).astype(summed.dtype)
    local_rows = summed.shape[2]
    summed = summed.reshape(circuits * spectator, local_rows, 2, width)
    amplitudes = lax.psum_scatter(
        summed.astype(jnp.bfloat16), "cuts", scatter_dimension=0, tiled=True
    ).astype(jnp.float32)
    row_count = amplitudes.shape[0]
    first_row = lax.axis_index("cuts") * row_count
    first_col = lax.axis_index("mode") * local_rows
    magnitude = amplitudes[:, :, 0, :] ** 2 + amplitudes[:, :, 1, :] ** 2
    row_sums = jnp.sum(magnitude, axis=(1, 2))
    owner_circuit = (first_row + jnp.arange(row_count, dtype=jnp.int32)) // spectator
    norm_part = jnp.sum(
        jnp.where(owner_circuit[None, :] == circuit_ids[:, None], row_sums[None, :], 0.0), axis=1
    )
    plane_size = width * width
    spec_index = samples // plane_size
    row_index = samples // width % width
    col_index = samples % width
    local_row = circuit_ids[:, None] * spectator + spec_index - first_row
    local_col = row_index - first_col
    is_owned = (
        (local_row >= 0) & (local_row < row_count) & (local_col >= 0) & (local_col < local_rows)
    )
    cell_index = jnp.where(is_owned, local_row * local_rows + local_col, -1)
    cell_count = row_count * local_rows
    cell_onehot = (
        cell_index[:, :, None] == jnp.arange(cell_count, dtype=jnp.int32)[None, None, :]
    ).astype(jnp.float32)
    picked_rows = jnp.einsum(
        "csr,rw->csw",
        cell_onehot,
        magnitude.reshape(cell_count, width),
        precision=lax.Precision.HIGHEST,
    )
    col_match = col_index[:, :, None] == jnp.arange(width, dtype=jnp.int32)[None, None, :]
    sample_mass = jnp.sum(jnp.where(col_match, picked_rows, 0.0), axis=2)
    dimension_scale = float(spectator * plane_size)
    norm_total = lax.psum(norm_part, ("cuts", "mode"))
    sample_probs = lax.psum(sample_mass * dimension_scale / norm_total[:, None], ("cuts", "mode"))
    xeb_score = jnp.mean(sample_probs, axis=1)
    return (amplitudes, sample_probs, xeb_score)


def solution(mesh):
    in_specs = (P(None, "cuts", None, "mode", None, None), P("cuts", None, None, None), P(), P())
    out_specs = (P("cuts", "mode", None, None), P(), P())
    return jax.shard_map(
        on_device, mesh=mesh, in_specs=in_specs, out_specs=out_specs, check_vma=False
    )
```

profile of v0, /device:TPU:0, one launch (start us, length us, event | category | flops | bytes accessed | tf_op | source)
XLA Modules:
  0.0 402.5 jit_solution(14701239896464762398)
XLA Ops:
  7.2 0.6 fusion.74
  10.4 1.6 fusion.73
  32.4 1.2 copy.56
  33.9 0.7 copy.39
  35.0 0.7 copy.40
  37.7 0.6 convert_select_fusion.5
  38.3 0.6 convert_select_fusion.4
  39.0 0.6 convert_select_fusion.3
  39.6 0.6 convert_select_fusion.2
  40.2 0.6 convert_select_fusion.1
  40.8 0.6 convert_select_fusion
  41.5 4.3 %all-to-all-start = ((bf16[8,2,4,32,2,128]{5,4,3,2,1,0:T(2,128)(2,1)}), bf16[8,2,4,32,2,128]{5,4,3,2,1,0:T(2,128)(2,1)S(1)}, u32[]{:S(2)}, u32[]{:S(2)}) async-start(bf16[8,2,4,32,2,128]{5,4,3,2,1,0:T(2,128)(2,1)} %param.4), calls=%async_computation | async-start | bytes 2097152 | tf_op jit(solution)/shard_map/all_to_all | solution.py:42
  45.8 72.8 %all-reduce.6.cloned.1.call-done = (bf16[1,2,128,128]{2,3,0,1:T(8,128)(2,1)}, bf16[1,2,128,128]{2,3,0,1:T(8,128)(2,1)}, bf16[1,2,128,128]{3,2,0,1:T(8,128)(2,1)}...) async-done(((bf16[1,2,128,128]{2,3,0,1:T(8,128)(2,1)}, ...) | async-done | bytes 524304 | tf_op jit(solution)/shard_map/psum | solution.py:9
  118.6 0.9 constant_dynamic-update-slice_fusion.1
  119.5 0.9 constant_dynamic-update-slice_fusion
  120.4 0.8 constant_dynamic-update-slice_fusion.3
  121.2 0.8 constant_dynamic-update-slice_fusion.5
  122.1 0.9 constant_dynamic-update-slice_fusion.2
  123.1 1.2 copy.55
  124.4 0.7 reshape.305
  125.1 0.5 fusion.2
  125.5 0.8 reshape.306
  126.3 1.1 copy.42
  127.4 0.7 reshape.307
  128.1 0.4 convolution_convert_fusion.2
  128.6 0.3 reshape.308
  128.9 1.2 copy.43
  130.1 0.7 reshape.309
  130.8 0.4 convolution_convert_fusion.1
  131.2 0.3 reshape.310
  131.5 1.2 copy.44
  132.8 0.7 reshape.311
  133.5 0.4 convolution_convert_fusion
  133.9 0.3 reshape.312
  134.2 2.4 reduce_sum.50
  136.7 0.7 copy.45
  137.4 11.4 %all_to_all.33 = bf16[2,4,128,2,128]{4,3,1,0,2:T(2,128)(2,1)S(1)} all-to-all(bf16[2,4,128,2,128]{4,3,1,0,2:T(2,128)(2,1)S(1)} %copy.45), channel_id=1, replica_groups=mesh['cuts'=8,'mode'=4] {'mode'}, dimensions={2} | all-to-all | bytes 1048576 | tf_op jit(solution)/shard_map/all_to_all | solution.py:66
  148.9 0.8 copy.47
  149.9 61.7 %reduce-scatter.2.cloned.1.call-done = bf16[4,32,2,128]{3,1,2,0:T(8,128)(2,1)} async-done(((bf16[32,32,2,128]{3,1,2,0:T(8,128)(2,1)}), bf16[4,32,2,128]{3,1,2,0:T(8,128)(2,1)}) %reduce-scatter.2.cloned.1.call-update) | async-done | bytes 65552 | tf_op jit(solution)/shard_map/reduce_scatter | solution.py:71
  211.5 0.8 convert_element_type.77
  212.9 40.1 %psum.78 = f32[8]{0:T(128)S(1)} all-reduce(f32[8]{0:T(128)S(1)} %select_reduce_fusion.1), channel_id=1, replica_groups=mesh['cuts'=8,'mode'=4] {'cuts','mode'}, use_global_device_ids=true, to_apply=%region_13.14 | all-reduce | flops 8 | bytes 64 | tf_op jit(solution)/shard_map/psum | solution.py:106
  252.9 15.4 %select_reduce_fusion = f32[8,4096]{1,0:T(8,128)S(1)} fusion(s32[8,4096]{1,0:T(8,128)S(1)} %get-tuple-element.23, f32[128,128,1]{1,0,2:T(8,128)S(1)} %bitcast.154, s32[8,4096]{1,0:T(8,128)S(1)} %get-tuple-element.22), kind=kOutput, calls=%fused_computation | convolution fusion | flops 6459195392 | bytes 458752 | tf_op jit(solution)/shard_map/csr,rw->csw/dot_general | solution.py:97
  268.4 0.7 multiply_divide_fusion
  269.2 0.7 copy.49
  269.9 123.0 %all-reduce.4.cloned.1.call-done = f32[8,4096]{1,0:T(8,128)} async-done(((f32[8,4096]{1,0:T(8,128)}), f32[8,4096]{1,0:T(8,128)}) %all-reduce.4.cloned.1.call-update) | async-done | bytes 131088 | tf_op jit(solution)/shard_map/psum | solution.py:107
  392.8 1.1 reduce_sum.55
  393.9 0.5 broadcast_multiply_fusion
  394.4 1.6 copy.70
  (42 shorter events, 3.2 us)
Async XLA Ops:
  7.2 111.4 %all-reduce.6.cloned.1.call-start = ((), (), s32[]{:S(2)}) async-start(), calls=%async_computation.5 | async-start | bytes 1048576 | tf_op jit(solution)/shard_map/psum | solution.py:9
  41.5 81.6 %all-to-all-start = ((bf16[8,2,4,32,2,128]{5,4,3,2,1,0:T(2,128)(2,1)}), bf16[8,2,4,32,2,128]{5,4,3,2,1,0:T(2,128)(2,1)S(1)}, u32[]{:S(2)}, u32[]{:S(2)}) async-start(bf16[8,2,4,32,2,128]{5,4,3,2,1,0:T(2,128)(2,1)} %param.4), calls=%async_computation | async-start | bytes 2097152 | tf_op jit(solution)/shard_map/all_to_all | solution.py:42
  45.8 165.8 %reduce-scatter.2.cloned.1.call-start = ((), (), s32[]{:S(2)}) async-start(), calls=%async_computation.3 | async-start | bytes 589824 | tf_op jit(solution)/shard_map/reduce_scatter | solution.py:71
  118.6 4.4 %copy-start.3 = (bf16[1,2,128,128]{3,2,0,1:T(8,128)(2,1)S(1)}, bf16[1,2,128,128]{3,2,0,1:T(8,128)(2,1)}, u32[]{:S(2)}) copy-start(bf16[1,2,128,128]{3,2,0,1:T(8,128)(2,1)} %get-tuple-element.18) | copy-start | bytes 196612
  118.6 4.4 %copy-start.2 = (bf16[1,2,128,128]{3,2,0,1:T(8,128)(2,1)S(1)}, bf16[1,2,128,128]{3,2,0,1:T(8,128)(2,1)}, u32[]{:S(2)}) copy-start(bf16[1,2,128,128]{3,2,0,1:T(8,128)(2,1)} %get-tuple-element.19) | copy-start | bytes 196612
  148.9 63.7 %copy-start.1 = (s32[8,4096]{1,0:T(8,128)S(1)}, s32[8,4096]{1,0:T(8,128)}, u32[]{:S(2)}) copy-start(s32[8,4096]{1,0:T(8,128)} %param.7) | copy-start | bytes 393220
  149.8 243.0 %all-reduce.4.cloned.1.call-start = ((), (), s32[]{:S(2)}) async-start(), calls=%async_computation.4 | async-start | bytes 262144 | tf_op jit(solution)/shard_map/psum | solution.py:107
  252.9 16.2 %copy-start = (bf16[4,32,2,128]{3,1,2,0:T(8,128)(2,1)S(1)}, bf16[4,32,2,128]{3,1,2,0:T(8,128)(2,1)}, u32[]{:S(2)}) copy-start(bf16[4,32,2,128]{3,1,2,0:T(8,128)(2,1)} %reduce-scatter.2.cloned.1.call-done) | copy-start | bytes 196612
Sparse Core Ops, SparseCore 0:
  41.6 76.9 all-reduce.5
  149.9 61.5 reduce-scatter.1
  269.3 123.5 all-reduce.3
where the time goes:
time: 403 us; the launch traced here: 402 us
  waiting for transfers between devices  257 us (64%)
  blocking collectives  51.4 us (13%)
  between operations  37.4 us (9%)
  local copies, waits for them, and re-layouts  22.5 us (6%)
  matrix products  19.5 us (5%)
  other arithmetic  9.91 us (2%)
  starting transfers between devices  4.36 us (1%)
    psum x1, waiting for transfers between devices, on_device(): lax.psum(sample_mass * dimension_scale / norm_total[:, None], ('cuts', 'm...  123 us
    psum x1, waiting for transfers between devices, from_root(): return lax.psum(jnp.where(mine, array, jnp.zeros_like(array)), axis)  72.8 us
    reduce_scatter x1, waiting for transfers between devices, on_device(): lax.psum_scatter(summed.astype(jnp.bfloat16), 'cuts', scatter_dimension=0...  61.7 us
    psum x1, blocking collectives, on_device(): norm_total = lax.psum(norm_part, ('cuts', 'mode'))  40.1 us
    dot_general x1, matrix products, on_device(): jnp.einsum('csr,rw->csw', cell_onehot, magnitude.reshape(cell_count, widt...  15.4 us
    all_to_all x1, blocking collectives, on_device(): lax.all_to_all(summed.astype(jnp.bfloat16), 'mode', split_axis=2, concat_...  11.4 us
  transfers between devices with their start and end apart: 4, of which 3 were waited for; matrix products, arithmetic and copies ran while one was open for 1% of the time, Pallas kernels for 0%

commit v1 on v0

--- a/solution.py
+++ b/solution.py
@@ -104,7 +104,9 @@
     sample_mass = jnp.sum(jnp.where(col_match, picked_rows, 0.0), axis=2)
     dimension_scale = float(spectator * plane_size)
     norm_total = lax.psum(norm_part, ("cuts", "mode"))
-    sample_probs = lax.psum(sample_mass * dimension_scale / norm_total[:, None], ("cuts", "mode"))
+    sample_probs = lax.psum(
+        lax.psum(sample_mass * dimension_scale / norm_total[:, None], "mode"), "cuts"
+    )
     xeb_score = jnp.mean(sample_probs, axis=1)
     return (amplitudes, sample_probs, xeb_score)
 

time: 403 us -> 384 us (0.953)
  waiting for transfers between devices: 257 us -> 238 us
    psum x1 -> x2, waiting for transfers between devices: 123 us -> 104 us  [the longest x1 73 us: on_device(): lax.psum(lax.psum(sample_mass * dimension_scale / norm_total[:, None], 'm...]
  transfers between devices with their start and end apart: 4 -> 5, of which waited for: 3 -> 4; matrix products, arithmetic and copies ran while one was open for 1% -> 1% of each run, Pallas kernels for 0% -> 0%
where the time goes in v1:
time: 384 us; the launch traced here: 383 us
  waiting for transfers between devices  238 us (62%)
  blocking collectives  51.4 us (13%)
  between operations  37.4 us (10%)
  local copies, waits for them, and re-layouts  22.5 us (6%)
  matrix products  19.5 us (5%)
  other arithmetic  9.91 us (3%)
  starting transfers between devices  4.4 us (1%)
    psum x1, waiting for transfers between devices, on_device(): lax.psum(lax.psum(sample_mass * dimension_scale / norm_total[:, None], 'm...  73 us
    psum x1, waiting for transfers between devices, from_root(): return lax.psum(jnp.where(mine, array, jnp.zeros_like(array)), axis)  72.8 us
    reduce_scatter x1, waiting for transfers between devices, on_device(): lax.psum_scatter(summed.astype(jnp.bfloat16), 'cuts', scatter_dimension=0...  61.7 us
    psum x1, blocking collectives, on_device(): norm_total = lax.psum(norm_part, ('cuts', 'mode'))  40.1 us
    psum x1, waiting for transfers between devices, on_device(): lax.psum(sample_mass * dimension_scale / norm_total[:, None], 'mode')  30.8 us
    dot_general x1, matrix products, on_device(): jnp.einsum('csr,rw->csw', cell_onehot, magnitude.reshape(cell_count, widt...  15.4 us
    all_to_all x1, blocking collectives, on_device(): lax.all_to_all(summed.astype(jnp.bfloat16), 'mode', split_axis=2, concat_...  11.4 us
  transfers between devices with their start and end apart: 5, of which 4 were waited for; matrix products, arithmetic and copies ran while one was open for 1% of the time, Pallas kernels for 0%

profile of v1, /device:TPU:0, one launch (start us, length us, event | category | flops | bytes accessed | tf_op | source)
XLA Modules:
  0.0 383.4 jit_solution(8037686019942547713)
XLA Ops:
  7.2 0.6 fusion.74
  10.4 1.6 fusion.73
  32.4 1.2 copy.56
  33.9 0.7 copy.39
  35.0 0.7 copy.40
  37.7 0.6 convert_select_fusion.5
  38.3 0.6 convert_select_fusion.4
  39.0 0.6 convert_select_fusion.3
  39.6 0.6 convert_select_fusion.2
  40.2 0.6 convert_select_fusion.1
  40.8 0.6 convert_select_fusion
  41.5 4.3 %all-to-all-start = ((bf16[8,2,4,32,2,128]{5,4,3,2,1,0:T(2,128)(2,1)}), bf16[8,2,4,32,2,128]{5,4,3,2,1,0:T(2,128)(2,1)S(1)}, u32[]{:S(2)}, u32[]{:S(2)}) async-start(bf16[8,2,4,32,2,128]{5,4,3,2,1,0:T(2,128)(2,1)} %param.4), calls=%async_computation | async-start | bytes 2097152 | tf_op jit(solution)/shard_map/all_to_all | solution.py:42
  45.8 72.8 %all-reduce.9.cloned.1.call-done = (bf16[1,2,128,128]{2,3,0,1:T(8,128)(2,1)}, bf16[1,2,128,128]{2,3,0,1:T(8,128)(2,1)}, bf16[1,2,128,128]{3,2,0,1:T(8,128)(2,1)}...) async-done(((bf16[1,2,128,128]{2,3,0,1:T(8,128)(2,1)}, ...) | async-done | bytes 524304 | tf_op jit(solution)/shard_map/psum | solution.py:9
  118.6 0.9 constant_dynamic-update-slice_fusion.1
  119.5 0.9 constant_dynamic-update-slice_fusion
  120.4 0.8 constant_dynamic-update-slice_fusion.3
  121.2 0.8 constant_dynamic-update-slice_fusion.5
  122.1 0.9 constant_dynamic-update-slice_fusion.2
  123.1 1.2 copy.55
  124.4 0.7 reshape.305
  125.1 0.5 fusion.2
  125.5 0.8 reshape.306
  126.3 1.1 copy.42
  127.4 0.7 reshape.307
  128.1 0.4 convolution_convert_fusion.2
  128.6 0.3 reshape.308
  128.9 1.2 copy.43
  130.1 0.7 reshape.309
  130.8 0.4 convolution_convert_fusion.1
  131.2 0.3 reshape.310
  131.5 1.2 copy.44
  132.8 0.7 reshape.311
  133.5 0.4 convolution_convert_fusion
  134.2 2.4 reduce_sum.50
  136.7 0.7 copy.45
  137.4 11.4 %all_to_all.33 = bf16[2,4,128,2,128]{4,3,1,0,2:T(2,128)(2,1)S(1)} all-to-all(bf16[2,4,128,2,128]{4,3,1,0,2:T(2,128)(2,1)S(1)} %copy.45), channel_id=1, replica_groups=mesh['cuts'=8,'mode'=4] {'mode'}, dimensions={2} | all-to-all | bytes 1048576 | tf_op jit(solution)/shard_map/all_to_all | solution.py:66
  148.9 0.8 copy.47
  149.9 61.7 %reduce-scatter.2.cloned.1.call-done = bf16[4,32,2,128]{3,1,2,0:T(8,128)(2,1)} async-done(((bf16[32,32,2,128]{3,1,2,0:T(8,128)(2,1)}), bf16[4,32,2,128]{3,1,2,0:T(8,128)(2,1)}) %reduce-scatter.2.cloned.1.call-update) | async-done | bytes 65552 | tf_op jit(solution)/shard_map/reduce_scatter | solution.py:71
  211.5 0.8 convert_element_type.77
  212.9 40.1 %psum.85 = f32[8]{0:T(128)S(1)} all-reduce(f32[8]{0:T(128)S(1)} %select_reduce_fusion.1), channel_id=1, replica_groups=mesh['cuts'=8,'mode'=4] {'cuts','mode'}, use_global_device_ids=true, to_apply=%region_13.14 | all-reduce | flops 8 | bytes 64 | tf_op jit(solution)/shard_map/psum | solution.py:106
  253.0 15.4 %select_reduce_fusion = f32[8,4096]{1,0:T(8,128)S(1)} fusion(s32[8,4096]{1,0:T(8,128)S(1)} %get-tuple-element.23, f32[128,128,1]{1,0,2:T(8,128)S(1)} %bitcast.154, s32[8,4096]{1,0:T(8,128)S(1)} %get-tuple-element.22), kind=kOutput, calls=%fused_computation | convolution fusion | flops 6459195392 | bytes 458752 | tf_op jit(solution)/shard_map/csr,rw->csw/dot_general | solution.py:97
  268.4 0.7 multiply_divide_fusion
  269.2 30.8 %all-reduce.5.cloned.1.call-done = f32[8,4096]{1,0:T(8,128)} async-done(((f32[8,4096]{1,0:T(8,128)}), f32[8,4096]{1,0:T(8,128)}) %all-reduce.5.cloned.1.call-update) | async-done | bytes 131088 | tf_op jit(solution)/shard_map/psum | solution.py:108
  300.1 0.7 copy.49
  300.8 73.0 %all-reduce.7.cloned.1.call-done = f32[8,4096]{1,0:T(8,128)} async-done(((f32[8,4096]{1,0:T(8,128)}), f32[8,4096]{1,0:T(8,128)}) %all-reduce.7.cloned.1.call-update) | async-done | bytes 131088 | tf_op jit(solution)/shard_map/psum | solution.py:107
  373.8 1.1 reduce_sum.55
  374.8 0.5 broadcast_multiply_fusion
  375.3 1.6 copy.71
  (45 shorter events, 3.5 us)
Async XLA Ops:
  7.2 111.4 %all-reduce.9.cloned.1.call-start = ((), (), s32[]{:S(2)}) async-start(), calls=%async_computation.6 | async-start | bytes 1048576 | tf_op jit(solution)/shard_map/psum | solution.py:9
  41.5 81.6 %all-to-all-start = ((bf16[8,2,4,32,2,128]{5,4,3,2,1,0:T(2,128)(2,1)}), bf16[8,2,4,32,2,128]{5,4,3,2,1,0:T(2,128)(2,1)S(1)}, u32[]{:S(2)}, u32[]{:S(2)}) async-start(bf16[8,2,4,32,2,128]{5,4,3,2,1,0:T(2,128)(2,1)} %param.4), calls=%async_computation | async-start | bytes 2097152 | tf_op jit(solution)/shard_map/all_to_all | solution.py:42
  45.8 165.8 %reduce-scatter.2.cloned.1.call-start = ((), (), s32[]{:S(2)}) async-start(), calls=%async_computation.3 | async-start | bytes 589824 | tf_op jit(solution)/shard_map/reduce_scatter | solution.py:71
  118.6 4.4 %copy-start.3 = (bf16[1,2,128,128]{3,2,0,1:T(8,128)(2,1)S(1)}, bf16[1,2,128,128]{3,2,0,1:T(8,128)(2,1)}, u32[]{:S(2)}) copy-start(bf16[1,2,128,128]{3,2,0,1:T(8,128)(2,1)} %get-tuple-element.18) | copy-start | bytes 196612
  118.6 4.4 %copy-start.2 = (bf16[1,2,128,128]{3,2,0,1:T(8,128)(2,1)S(1)}, bf16[1,2,128,128]{3,2,0,1:T(8,128)(2,1)}, u32[]{:S(2)}) copy-start(bf16[1,2,128,128]{3,2,0,1:T(8,128)(2,1)} %get-tuple-element.19) | copy-start | bytes 196612
  148.9 63.7 %copy-start.1 = (s32[8,4096]{1,0:T(8,128)S(1)}, s32[8,4096]{1,0:T(8,128)}, u32[]{:S(2)}) copy-start(s32[8,4096]{1,0:T(8,128)} %param.7) | copy-start | bytes 393220
  149.8 150.3 %all-reduce.5.cloned.1.call-start = ((), (), s32[]{:S(2)}) async-start(), calls=%async_computation.4 | async-start | bytes 262144 | tf_op jit(solution)/shard_map/psum | solution.py:108
  253.0 47.1 %copy-start = (bf16[4,32,2,128]{3,1,2,0:T(8,128)(2,1)S(1)}, bf16[4,32,2,128]{3,1,2,0:T(8,128)(2,1)}, u32[]{:S(2)}) copy-start(bf16[4,32,2,128]{3,1,2,0:T(8,128)(2,1)} %reduce-scatter.2.cloned.1.call-done) | copy-start | bytes 196612
  269.2 104.6 %all-reduce.7.cloned.1.call-start = ((), (), s32[]{:S(2)}) async-start(), calls=%async_computation.5 | async-start | bytes 262144 | tf_op jit(solution)/shard_map/psum | solution.py:107
Sparse Core Ops, SparseCore 0:
  41.6 76.9 all-reduce.8
  149.9 61.5 reduce-scatter.1
  269.3 30.7 all-reduce.4
  303.3 70.4 all-reduce.6
